TPU v7x, 128 devices: a whole 4x4x4 slice. The times are simulated.
128 devices in a mesh: blk: 8 (over y, x_lo), inner: 16 (over z, x_hi, core).
Axes of the slice: x: 4 (x_hi: 2, x_lo: 2; x = x_hi * 2 + x_lo), y: 4, z: 4, core: 2. Of those that a mesh axis runs over, the one named last changes fastest.
Arguments:
- points: float32 [16384, 128], P(('blk', 'inner')), may hold values from -8 to 8
- lengthscales: float32 [128], replicated, may hold values from 6 to 24
- noise_level: float32 [1], replicated, may hold values from 1 to 10
- iterate: float32 [16384, 64], P(('blk', 'inner')), may hold values from -6 to 6
- residual: float32 [16384, 64], P(('blk', 'inner')), may hold values from -6 to 6
- direction: float32 [16384, 64], P(('blk', 'inner')), may hold values from -6 to 6
Outputs:
- new_iterate: float32 [16384, 64], P(('blk', 'inner'))
- new_residual: float32 [16384, 64], P(('blk', 'inner'))
- new_direction: float32 [16384, 64], P(('blk', 'inner'))
All inputs are finite; a program needn't handle non-finite values.
Results may differ from a plain program's by a relative error of at most 0.00014.
Values sent between devices are 32-bit elements; how exact they have to be, the bound alone decides.
No kernel may reach another device: no remote copies, remote signals or barrier semaphores. Data moves between devices by JAX's collectives and lax.ppermute only.
A program may use at most 64 MiB of HBM per device.

v0:
```python
import jax
import jax.numpy as jnp
from jax import lax
from jax.sharding import PartitionSpec as P


def sent_together(arrays, axis, dim, along):
    both = jnp.concatenate(arrays, axis=along)
    whole, at, outs = (lax.all_gather(both, axis, axis=dim, tiled=True), 0, [])
    for a in arrays:
        outs.append(lax.slice_in_dim(whole, at, at + a.shape[along], axis=along))
        at += a.shape[along]
    return tuple(outs)


def from_behind(value, axis, by):
    size = lax.axis_size(axis)
    return lax.ppermute(value, axis, [(i, (i + by) % size) for i in range(size)])


def split_up(value, dim, size):
    dims = value.shape
    blocks = value.reshape(*dims[:dim], size, dims[dim] // size, *dims[dim + 1 :])
    return jnp.moveaxis(blocks, dim, 0)


def sum_at_owner(value, axis, dim):
    size = lax.axis_size(axis)
    blocks = lax.all_to_all(split_up(value, dim, size), axis, 0, 0, tiled=True)
    return jnp.sum(blocks, axis=0)


def kernel_block(left, left_sq, right, right_sq):
    products = lax.dot_general(
        left,
        right,
        (((1,), (1,)), ((), ())),
        precision=lax.Precision.HIGHEST,
        preferred_element_type=jnp.float32,
    )
    return jnp.exp(-0.5 * (left_sq[:, None] + right_sq[None, :] - 2.0 * products))


def matmul(left, right):
    return jnp.dot(left, right, precision=lax.Precision.HIGHEST, preferred_element_type=jnp.float32)


def transposed(left, right):
    return lax.dot_general(
        left,
        right,
        (((0,), (0,)), ((), ())),
        precision=lax.Precision.HIGHEST,
        preferred_element_type=jnp.float32,
    )


def chol_solve(matrix, rhs_side):
    factor = jnp.linalg.cholesky(matrix)
    return jax.scipy.linalg.cho_solve((factor, True), rhs_side)


def on_device(points, lengthscales, noise_level, iterate, residual, direction):
    scaled = points / lengthscales[None, :]
    sq_norms = jnp.sum(scaled * scaled, axis=1)
    cycle_size = lax.axis_size("blk")
    group_pts, group_dir = sent_together((scaled, direction), "inner", 0, 1)
    group_sq = jnp.sum(group_pts * group_pts, axis=1)
    partial_value = jnp.zeros((group_pts.shape[0], direction.shape[1]), jnp.float32)
    halfway = cycle_size // 2
    visitor = (scaled, sq_norms, direction, jnp.zeros_like(direction))
    returned = jnp.zeros_like(direction)
    for offset in range(halfway + 1):
        if offset > 0:
            visitor = from_behind((visitor[0], visitor[1], visitor[2], visitor[3]), "blk", 1)
        kernel_tile = kernel_block(group_pts, group_sq, visitor[0], visitor[1])
        partial_value = partial_value + matmul(kernel_tile, visitor[2])
        if 1 <= offset <= halfway - 1:
            carried = visitor[3] + transposed(kernel_tile, group_dir)
            visitor = (visitor[0], visitor[1], visitor[2], carried)
            if offset == halfway - 1:
                returned = from_behind(carried, "blk", -(halfway - 1))
    owned = sum_at_owner(partial_value, "inner", 0)
    image = owned + returned + noise_level[0] * direction
    local_gram = transposed(direction, image)
    local_res = transposed(residual, residual)
    local_cross = transposed(image, residual)
    local_image = transposed(image, image)
    gram_raw, res_gram, cross_gram, image_gram = lax.psum(
        (local_gram, local_res, local_cross, local_image), ("blk", "inner")
    )
    gram_matrix = 0.5 * (gram_raw + gram_raw.T)
    step_size = chol_solve(gram_matrix, res_gram)
    new_residual = residual - matmul(image, step_size)
    cross_term = transposed(step_size, cross_gram)
    new_gram = (
        res_gram - cross_term - cross_term.T + transposed(step_size, matmul(image_gram, step_size))
    )
    new_iterate = iterate + matmul(direction, step_size)
    correction = chol_solve(res_gram, new_gram)
    new_direction = new_residual + matmul(direction, correction)
    return (new_iterate, new_residual, new_direction)


def solution(mesh):
    return jax.shard_map(
        on_device,
        mesh=mesh,
        in_specs=(
            P(("blk", "inner"), None),
            P(),
            P(),
            P(("blk", "inner"), None),
            P(("blk", "inner"), None),
            P(("blk", "inner"), None),
        ),
        out_specs=(P(("blk", "inner"), None), P(("blk", "inner"), None), P(("blk", "inner"), None)),
        check_vma=False,
    )
```

profile of v0, /device:TPU:0, one launch (start us, length us, event | category | flops | bytes accessed | tf_op | source)
XLA Modules:
  0.0 288.0 jit_solution(3452829028754681316)
XLA Ops:
  7.2 0.8 copy.16
  8.1 1.0 multiply_reduce_fusion.1
  9.7 1.7 collective-permute-start.1
  11.4 4.8 %collective-permute-done.1 = f32[128,128]{1,0:T(8,128)S(1)} collective-permute-done((f32[128,128]{1,0:T(8,128)S(1)}, f32[128,128]{1,0:T(8,128)S(1)}, u32[]{:S(2)}, u32[]{:S(2)}) %collective-permute-start.1) | collective-permute-done | bytes 65568 | tf_op jit(solution)/shard_map/ppermute | solution.py:18
  16.2 1.9 collective-permute-start.2
  18.1 4.8 %collective-permute-done.2 = f32[128,64]{0,1:T(8,128)S(1)} collective-permute-done((f32[128,64]{0,1:T(8,128)}, f32[128,64]{0,1:T(8,128)S(1)}, u32[]{:S(2)}, u32[]{:S(2)}) %collective-permute-start.2) | collective-permute-done | bytes 32800 | tf_op jit(solution)/shard_map/ppermute | solution.py:18
  22.9 0.8 collective-permute-start.7
  23.7 5.5 %collective-permute-done.5 = f32[128,64]{0,1:T(8,128)S(1)} collective-permute-done((f32[128,64]{0,1:T(8,128)S(1)}, f32[128,64]{0,1:T(8,128)S(1)}, u32[]{:S(2)}, u32[]{:S(2)}) %collective-permute-start.5) | collective-permute-done | bytes 32800 | tf_op jit(solution)/shard_map/ppermute | solution.py:18
  29.3 6.1 %collective-permute-done = f32[128]{0:T(128)S(1)} collective-permute-done((f32[128]{0:T(128)S(1)}, f32[128]{0:T(128)S(1)}, u32[]{:S(2)}, u32[]{:S(2)}) %collective-permute-start) | collective-permute-done | bytes 544 | tf_op jit(solution)/shard_map/ppermute | solution.py:18
  35.4 5.7 %collective-permute-done.3 = f32[128]{0:T(128)S(1)} collective-permute-done((f32[128]{0:T(128)S(1)}, f32[128]{0:T(128)S(1)}, u32[]{:S(2)}, u32[]{:S(2)}) %collective-permute-start.3) | collective-permute-done | bytes 544 | tf_op jit(solution)/shard_map/ppermute | solution.py:18
  41.1 5.7 %collective-permute-done.6 = f32[128]{0:T(128)S(1)} collective-permute-done((f32[128]{0:T(128)S(1)}, f32[128]{0:T(128)S(1)}, u32[]{:S(2)}, u32[]{:S(2)}) %collective-permute-start.6) | collective-permute-done | bytes 544 | tf_op jit(solution)/shard_map/ppermute | solution.py:18
  46.8 14.3 %all-gather.2.cloned.1.call-done = f32[2048,192]{1,0:T(8,128)} async-done(((f32[128,192]{1,0:T(8,128)}), f32[2048,192]{1,0:T(8,128)}) %all-gather.2.cloned.1.call-update) | async-done | bytes 1572880 | tf_op jit(solution)/shard_map/all_gather | solution.py:9
  61.2 1.7 multiply_reduce_fusion
  62.9 2.2 convolution_multiply_fusion.3
  65.2 1.1 fusion.2
  66.2 1.3 fusion.67
  67.5 2.2 convolution_add_fusion.5
  69.7 2.0 collective-permute-start.13
  71.7 1.0 convolution_multiply_fusion.1
  72.7 1.0 convolution_multiply_fusion.2
  73.7 1.0 convolution_multiply_fusion
  74.7 1.5 convolution_add_fusion.3
  76.2 1.5 convolution_add_fusion.2
  77.7 1.5 convolution_add_fusion.1
  79.2 2.2 fusion.15
  81.4 2.5 collective-permute-start.14
  83.8 1.5 fusion.3
  85.3 0.9 copy.28
  86.2 4.2 %all-to-all-start = ((f32[16,128,64]{1,2,0:T(8,128)}), f32[16,128,64]{1,2,0:T(8,128)}, u32[]{:S(2)}, u32[]{:S(2)}) async-start(f32[16,128,64]{1,2,0:T(8,128)} %bitcast.82), calls=%async_computation | async-start | bytes 1048576 | tf_op jit(solution)/shard_map/all_to_all | solution.py:29
  90.7 2.2 fusion.18
  92.9 2.1 collective-permute-start.15
  95.1 0.8 fusion.68
  96.5 6.6 %all-to-all-done = f32[16,128,64]{1,2,0:T(8,128)} async-done(((f32[16,128,64]{1,2,0:T(8,128)}), f32[16,128,64]{1,2,0:T(8,128)}, u32[]{:S(2)}, u32[]{:S(2)}) %all-to-all-start) | async-done | bytes 524320 | tf_op jit(solution)/shard_map/all_to_all | solution.py:29
  103.1 1.1 reduce_sum.29
  104.2 0.8 fusion.71
  106.7 140.5 %all-reduce.3.cloned.1.call-done = (f32[64,64]{0,1:T(8,128)}, f32[64,64]{1,0:T(8,128)}, f32[64,64]{1,0:T(8,128)}, f32[64,64]{1,0:T(8,128)}) async-done(((f32[64,64]{0,1:T(8,128)}, f32[64,64]{1,0:T(8,128)}, f32[64,64]{1,0:T(8,128)}, f32[64,64]{1,0:T(8,128)}), (f32[64,64]{0,1:T(8,128)}, f32[64,64]{1,0:T(8,128)}, f32[64,64]{1,0:T(8,128)}, f32[64,64]{1,0:T(8,128)})) %all-reduce.3.cloned.1.call-update) | async-done | bytes 65552 | tf_op jit(solution)/shard_map/psum | solution.py:89
  247.1 0.8 copy.19
  248.8 5.8 %cholesky.44 = f32[64,64]{1,0:T(8,128)S(1)} custom-call(f32[64,64]{1,0:T(8,128)S(1)} %fusion.58), custom_call_target="Cholesky" | custom-call | tf_op jit(solution)/shard_map/jit(cholesky)/cholesky | solution.py:59
  256.0 4.9 %custom-call.8 = f32[1,64,64]{1,2,0:T(8,128)S(1)} custom-call(f32[1,64,64]{2,1,0:T(8,128)S(1)} %fusion.47), custom_call_target="InvertDiagBlocksLowerTriangular" | custom-call | tf_op jit(solution)/shard_map/jit(_cho_solve)/triangular_solve | solution.py:60
  260.9 0.8 copy.22
  261.7 1.0 fusion.56
  263.2 1.0 fusion.70
  264.2 0.9 fusion.72
  265.2 0.9 fusion.5
  266.8 5.8 %cholesky.55 = f32[64,64]{1,0:T(8,128)S(1)} custom-call(f32[64,64]{1,0:T(8,128)S(1)} %fusion.53), custom_call_target="Cholesky" | custom-call | tf_op jit(solution)/shard_map/jit(cholesky)/cholesky | solution.py:59
  274.0 4.9 %custom-call.9 = f32[1,64,64]{1,2,0:T(8,128)S(1)} custom-call(f32[1,64,64]{2,1,0:T(8,128)S(1)} %fusion.48), custom_call_target="InvertDiagBlocksLowerTriangular" | custom-call | tf_op jit(solution)/shard_map/jit(_cho_solve)/triangular_solve | solution.py:60
  278.9 1.0 convolution_add_fusion.4
  280.3 0.9 fusion.4
  (54 shorter events, 7.9 us)
Async XLA Ops:
  7.2 54.0 %all-gather.2.cloned.1.call-start = ((), (), s32[]{:S(2)}) async-start(), calls=%async_computation.1 | async-start | bytes 2228224 | tf_op jit(solution)/shard_map/all_gather | solution.py:9
  9.7 6.4 %collective-permute-start.1 = (f32[128,128]{1,0:T(8,128)S(1)}, f32[128,128]{1,0:T(8,128)S(1)}, u32[]{:S(2)}, u32[]{:S(2)}) collective-permute-start(f32[128,128]{1,0:T(8,128)S(1)} %get-tuple-element.10), channel_id=1, source_target_pairs={{0,16},{16,32},{32,48},{48,64},{64,80},{80,96},{96,112},{112,0},{1... | collective-permute-start | bytes 196616 | tf_op jit(solution)/shard_map/ppermute | solution.py:18
  16.2 6.7 %collective-permute-start.4 = (f32[128,128]{1,0:T(8,128)S(1)}, f32[128,128]{1,0:T(8,128)S(1)}, u32[]{:S(2)}, u32[]{:S(2)}) collective-permute-start(f32[128,128]{1,0:T(8,128)S(1)} %collective-permute-done.1), channel_id=1, source_target_pairs={{0,16},{16,32},{32,48},{48,64},{64,80},{80,96},{96,112},{112,0},{1... | collective-permute-start | bytes 196616 | tf_op jit(solution)/shard_map/ppermute | solution.py:18
  16.2 6.7 %collective-permute-start.2 = (f32[128,64]{0,1:T(8,128)}, f32[128,64]{0,1:T(8,128)S(1)}, u32[]{:S(2)}, u32[]{:S(2)}) collective-permute-start(f32[128,64]{0,1:T(8,128)} %param.14), channel_id=1, source_target_pairs={{0,16},{16,32},{32,48},{48,64},{64,80},{80,96},{96,112},{112,0},{1... | collective-permute-start | bytes 98312 | tf_op jit(solution)/shard_map/ppermute | solution.py:18
  22.9 6.4 %collective-permute-start.5 = (f32[128,64]{0,1:T(8,128)S(1)}, f32[128,64]{0,1:T(8,128)S(1)}, u32[]{:S(2)}, u32[]{:S(2)}) collective-permute-start(f32[128,64]{0,1:T(8,128)S(1)} %collective-permute-done.2), channel_id=1, source_target_pairs={{0,16},{16,32},{32,48},{48,64},{64,80},{80,96},{96,112},{112,0},{1... | collective-permute-start | bytes 98312 | tf_op jit(solution)/shard_map/ppermute | solution.py:18
  22.9 23.9 %collective-permute-start.7 = (f32[128,128]{1,0:T(8,128)S(1)}, f32[128,128]{1,0:T(8,128)S(1)}, u32[]{:S(2)}, u32[]{:S(2)}) collective-permute-start(f32[128,128]{1,0:T(8,128)S(1)} %collective-permute-done.4), channel_id=1, source_target_pairs={{0,16},{16,32},{32,48},{48,64},{64,80},{80,96},{96,112},{112,0},{1... | collective-permute-start | bytes 196616 | tf_op jit(solution)/shard_map/ppermute | solution.py:18
  29.3 17.5 %collective-permute-start.8 = (f32[128,64]{0,1:T(8,128)S(1)}, f32[128,64]{0,1:T(8,128)S(1)}, u32[]{:S(2)}, u32[]{:S(2)}) collective-permute-start(f32[128,64]{0,1:T(8,128)S(1)} %collective-permute-done.5), channel_id=1, source_target_pairs={{0,16},{16,32},{32,48},{48,64},{64,80},{80,96},{96,112},{112,0},{1... | collective-permute-start | bytes 98312 | tf_op jit(solution)/shard_map/ppermute | solution.py:18
  29.3 6.1 %collective-permute-start = (f32[128]{0:T(128)S(1)}, f32[128]{0:T(128)S(1)}, u32[]{:S(2)}, u32[]{:S(2)}) collective-permute-start(f32[128]{0:T(128)S(1)} %get-tuple-element.9), channel_id=1, source_target_pairs={{0,16},{16,32},{32,48},{48,64},{64,80},{80,96},{96,112},{112,0},{1... | collective-permute-start | bytes 1544 | tf_op jit(solution)/shard_map/ppermute | solution.py:18
  35.4 5.7 %collective-permute-start.3 = (f32[128]{0:T(128)S(1)}, f32[128]{0:T(128)S(1)}, u32[]{:S(2)}, u32[]{:S(2)}) collective-permute-start(f32[128]{0:T(128)S(1)} %collective-permute-done), channel_id=1, source_target_pairs={{0,16},{16,32},{32,48},{48,64},{64,80},{80,96},{96,112},{112,0},{1... | collective-permute-start | bytes 1544 | tf_op jit(solution)/shard_map/ppermute | solution.py:18
  41.1 5.7 %collective-permute-start.6 = (f32[128]{0:T(128)S(1)}, f32[128]{0:T(128)S(1)}, u32[]{:S(2)}, u32[]{:S(2)}) collective-permute-start(f32[128]{0:T(128)S(1)} %collective-permute-done.3), channel_id=1, source_target_pairs={{0,16},{16,32},{32,48},{48,64},{64,80},{80,96},{96,112},{112,0},{1... | collective-permute-start | bytes 1544 | tf_op jit(solution)/shard_map/ppermute | solution.py:18
  41.1 26.4 %collective-permute-start.12 = (f32[128,64]{0,1:T(8,128)S(1)}, f32[128,64]{0,1:T(8,128)S(1)}, u32[]{:S(2)}, u32[]{:S(2)}) collective-permute-start(f32[128,64]{0,1:T(8,128)S(1)} %broadcast_in_dim.2), channel_id=1, source_target_pairs={{0,16},{16,32},{32,48},{48,64},{64,80},{80,96},{96,112},{112,0},{1... | collective-permute-start | bytes 98312 | tf_op jit(solution)/shard_map/ppermute | solution.py:18
  46.7 37.1 %collective-permute-start.9 = (f32[128]{0:T(128)S(1)}, f32[128]{0:T(128)S(1)}, u32[]{:S(2)}, u32[]{:S(2)}) collective-permute-start(f32[128]{0:T(128)S(1)} %collective-permute-done.6), channel_id=1, source_target_pairs={{0,16},{16,32},{32,48},{48,64},{64,80},{80,96},{96,112},{112,0},{1... | collective-permute-start | bytes 1544 | tf_op jit(solution)/shard_map/ppermute | solution.py:18
  46.7 37.1 %collective-permute-start.11 = (f32[128,64]{0,1:T(8,128)S(1)}, f32[128,64]{0,1:T(8,128)S(1)}, u32[]{:S(2)}, u32[]{:S(2)}) collective-permute-start(f32[128,64]{0,1:T(8,128)S(1)} %collective-permute-done.8), channel_id=1, source_target_pairs={{0,16},{16,32},{32,48},{48,64},{64,80},{80,96},{96,112},{112,0},{1... | collective-permute-start | bytes 98312 | tf_op jit(solution)/shard_map/ppermute | solution.py:18
  46.8 26.9 %collective-permute-start.10 = (f32[128,128]{1,0:T(8,128)S(1)}, f32[128,128]{1,0:T(8,128)S(1)}, u32[]{:S(2)}, u32[]{:S(2)}) collective-permute-start(f32[128,128]{1,0:T(8,128)S(1)} %collective-permute-done.7), channel_id=1, source_target_pairs={{0,16},{16,32},{32,48},{48,64},{64,80},{80,96},{96,112},{112,0},{1... | collective-permute-start | bytes 196616 | tf_op jit(solution)/shard_map/ppermute | solution.py:18
  61.2 4.0 %copy-start = (f32[2048,192]{1,0:T(8,128)S(1)}, f32[2048,192]{1,0:T(8,128)}, u32[]{:S(2)}) copy-start(f32[2048,192]{1,0:T(8,128)} %all-gather.2.cloned.1.call-done) | copy-start | bytes 4718596
  62.9 3.3 %copy-start.1 = (f32[128,64]{0,1:T(8,128)S(1)}, f32[128,64]{0,1:T(8,128)}, u32[]{:S(2)}) copy-start(f32[128,64]{0,1:T(8,128)} %param.14) | copy-start | bytes 98308
  69.7 9.5 %collective-permute-start.13 = (f32[128,64]{0,1:T(8,128)S(1)}, f32[128,64]{0,1:T(8,128)S(1)}, u32[]{:S(2)}, u32[]{:S(2)}) collective-permute-start(f32[128,64]{0,1:T(8,128)S(1)} %convolution_add_fusion.5), channel_id=1, source_target_pairs={{0,16},{16,32},{32,48},{48,64},{64,80},{80,96},{96,112},{112,0},{1... | collective-permute-start | bytes 98312 | tf_op jit(solution)/shard_map/ppermute | solution.py:18
  81.4 9.4 %collective-permute-start.14 = (f32[128,64]{0,1:T(8,128)S(1)}, f32[128,64]{0,1:T(8,128)S(1)}, u32[]{:S(2)}, u32[]{:S(2)}) collective-permute-start(f32[128,64]{0,1:T(8,128)S(1)} %fusion.15), channel_id=1, source_target_pairs={{0,16},{16,32},{32,48},{48,64},{64,80},{80,96},{96,112},{112,0},{1... | collective-permute-start | bytes 98312 | tf_op jit(solution)/shard_map/ppermute | solution.py:18
  85.3 9.7 %copy-start.2 = (f32[128,64]{0,1:T(8,128)S(1)}, f32[128,64]{0,1:T(8,128)}, u32[]{:S(2)}) copy-start(f32[128,64]{0,1:T(8,128)} %param.13) | copy-start | bytes 98308
  86.2 16.9 %all-to-all-start = ((f32[16,128,64]{1,2,0:T(8,128)}), f32[16,128,64]{1,2,0:T(8,128)}, u32[]{:S(2)}, u32[]{:S(2)}) async-start(f32[16,128,64]{1,2,0:T(8,128)} %bitcast.82), calls=%async_computation | async-start | bytes 1048576 | tf_op jit(solution)/shard_map/all_to_all | solution.py:29
  90.4 174.7 %copy-start.4 = (f32[128,64]{0,1:T(8,128)S(1)}, f32[128,64]{0,1:T(8,128)}, u32[]{:S(2)}) copy-start(f32[128,64]{0,1:T(8,128)} %param.12) | copy-start | bytes 98308
  90.5 156.7 %all-reduce.3.cloned.1.call-start = ((), (), s32[]{:S(2)}) async-start(), calls=%async_computation.2 | async-start | bytes 262144 | tf_op jit(solution)/shard_map/psum | solution.py:89
  92.9 11.3 %collective-permute-start.15 = (f32[128,64]{0,1:T(8,128)S(1)}, f32[128,64]{0,1:T(8,128)S(1)}, u32[]{:S(2)}, u32[]{:S(2)}) collective-permute-start(f32[128,64]{0,1:T(8,128)S(1)} %fusion.18), channel_id=1, source_target_pairs={{0,80},{16,96},{32,112},{48,0},{64,16},{80,32},{96,48},{112,64},{1... | collective-permute-start | bytes 98312 | tf_op jit(solution)/shard_map/ppermute | solution.py:18
  263.2 18.0 %copy-start.3 = (f32[128,64]{0,1:T(8,128)}, f32[128,64]{0,1:T(8,128)S(1)}, u32[]{:S(2)}) copy-start(f32[128,64]{0,1:T(8,128)S(1)} %convolution_subtract_fusion) | copy-start | bytes 98308
Sparse Core Ops, SparseCore 0:
  10.4 50.6 all-gather.1
  106.8 140.2 all-reduce.2
where the time goes:
time: 289 us; the launch traced here: 288 us
  waiting for transfers between devices  194 us (67%)
  other arithmetic  30.1 us (10%)
  matrix products  29.6 us (10%)
  starting transfers between devices  15.7 us (5%)
  between operations  15 us (5%)
  local copies, waits for them, and re-layouts  3.56 us (1%)
    psum x1, waiting for transfers between devices, on_device(): lax.psum((local_gram, local_res, local_cross, local_image), ('blk', 'inne...  140 us
    ppermute x16, waiting for transfers between devices, from_behind(): lax.ppermute(value, axis, [(i, (i + by) % size) for i in range(size)])  32.6 us
    all_gather x1, waiting for transfers between devices, sent_together(): whole, at, outs = (lax.all_gather(both, axis, axis=dim, tiled=True), 0, [])  14.3 us
    another operation x6, other arithmetic, chol_solve(): factor = jnp.linalg.cholesky(matrix)  13 us
    dot_general x9, matrix products, transposed(): lax.dot_general(left, right, (((0,), (0,)), ((), ())), precision=lax.Prec...  11.7 us
    ppermute x16, starting transfers between devices, from_behind(): lax.ppermute(value, axis, [(i, (i + by) % size) for i in range(size)])  11.1 us
    another operation x4, other arithmetic, chol_solve(): return jax.scipy.linalg.cho_solve((factor, True), rhs_side)  11.1 us
    dot_general x9, matrix products, matmul(): jnp.dot(left, right, precision=lax.Precision.HIGHEST, preferred_element_t...  10.2 us
  transfers between devices with their start and end apart: 19, of which 9 were waited for; matrix products, arithmetic and copies ran while one was open for 8% of the time, Pallas kernels for 0%

commit v1 on v0

--- a/solution.py
+++ b/solution.py
@@ -86,8 +86,13 @@
     local_res = transposed(residual, residual)
     local_cross = transposed(image, residual)
     local_image = transposed(image, image)
-    gram_raw, res_gram, cross_gram, image_gram = lax.psum(
-        (local_gram, local_res, local_cross, local_image), ("blk", "inner")
+
+    def process_the_case(unit, group_axis, across):
+        w2 = lax.psum(unit, group_axis)
+        return lax.psum(w2, across)
+
+    gram_raw, res_gram, cross_gram, image_gram = process_the_case(
+        (local_gram, local_res, local_cross, local_image), "inner", "blk"
     )
     gram_matrix = 0.5 * (gram_raw + gram_raw.T)
     step_size = chol_solve(gram_matrix, res_gram)

time: 289 us -> 361 us (1.25)
  waiting for transfers between devices: 194 us -> 267 us
    psum x1 -> x2, waiting for transfers between devices: 140 us -> 213 us  [the longest x1 135 us: process_the_case(): w2 = lax.psum(unit, group_axis)]
  transfers between devices with their start and end apart: 19 -> 20, of which waited for: 9 -> 10; matrix products, arithmetic and copies ran while one was open for 8% -> 7% of each run, Pallas kernels for 0% -> 0%
where the time goes in v1:
time: 361 us; the launch traced here: 360 us
  waiting for transfers between devices  267 us (74%)
  other arithmetic  30.1 us (8%)
  matrix products  29.6 us (8%)
  starting transfers between devices  15.7 us (4%)
  between operations  14.7 us (4%)
    psum x1, waiting for transfers between devices, process_the_case(): w2 = lax.psum(unit, group_axis)  135 us
    psum x1, waiting for transfers between devices, process_the_case(): return lax.psum(w2, across)  77.6 us
    ppermute x16, waiting for transfers between devices, from_behind(): lax.ppermute(value, axis, [(i, (i + by) % size) for i in range(size)])  32.6 us
    all_gather x1, waiting for transfers between devices, sent_together(): whole, at, outs = (lax.all_gather(both, axis, axis=dim, tiled=True), 0, [])  14.3 us
    another operation x6, other arithmetic, chol_solve(): factor = jnp.linalg.cholesky(matrix)  13 us
    dot_general x9, matrix products, transposed(): lax.dot_general(left, right, (((0,), (0,)), ((), ())), precision=lax.Prec...  11.7 us
    ppermute x16, starting transfers between devices, from_behind(): lax.ppermute(value, axis, [(i, (i + by) % size) for i in range(size)])  11.1 us
    another operation x4, other arithmetic, chol_solve(): return jax.scipy.linalg.cho_solve((factor, True), rhs_side)  11.1 us
  transfers between devices with their start and end apart: 20, of which 10 were waited for; matrix products, arithmetic and copies ran while one was open for 7% of the time, Pallas kernels for 0%

profile of v1, /device:TPU:0, one launch (start us, length us, event | category | flops | bytes accessed | tf_op | source)
XLA Modules:
  0.0 360.4 jit_solution(1572929728527310335)
XLA Ops:
  7.2 0.8 copy.16
  8.1 1.0 multiply_reduce_fusion.1
  9.7 1.7 collective-permute-start.1
  11.4 4.8 %collective-permute-done.1 = f32[128,128]{1,0:T(8,128)S(1)} collective-permute-done((f32[128,128]{1,0:T(8,128)S(1)}, f32[128,128]{1,0:T(8,128)S(1)}, u32[]{:S(2)}, u32[]{:S(2)}) %collective-permute-start.1) | collective-permute-done | bytes 65568 | tf_op jit(solution)/shard_map/ppermute | solution.py:18
  16.2 1.9 collective-permute-start.2
  18.1 4.8 %collective-permute-done.2 = f32[128,64]{0,1:T(8,128)S(1)} collective-permute-done((f32[128,64]{0,1:T(8,128)}, f32[128,64]{0,1:T(8,128)S(1)}, u32[]{:S(2)}, u32[]{:S(2)}) %collective-permute-start.2) | collective-permute-done | bytes 32800 | tf_op jit(solution)/shard_map/ppermute | solution.py:18
  22.9 0.8 collective-permute-start.7
  23.7 5.5 %collective-permute-done.5 = f32[128,64]{0,1:T(8,128)S(1)} collective-permute-done((f32[128,64]{0,1:T(8,128)S(1)}, f32[128,64]{0,1:T(8,128)S(1)}, u32[]{:S(2)}, u32[]{:S(2)}) %collective-permute-start.5) | collective-permute-done | bytes 32800 | tf_op jit(solution)/shard_map/ppermute | solution.py:18
  29.3 6.1 %collective-permute-done = f32[128]{0:T(128)S(1)} collective-permute-done((f32[128]{0:T(128)S(1)}, f32[128]{0:T(128)S(1)}, u32[]{:S(2)}, u32[]{:S(2)}) %collective-permute-start) | collective-permute-done | bytes 544 | tf_op jit(solution)/shard_map/ppermute | solution.py:18
  35.4 5.7 %collective-permute-done.3 = f32[128]{0:T(128)S(1)} collective-permute-done((f32[128]{0:T(128)S(1)}, f32[128]{0:T(128)S(1)}, u32[]{:S(2)}, u32[]{:S(2)}) %collective-permute-start.3) | collective-permute-done | bytes 544 | tf_op jit(solution)/shard_map/ppermute | solution.py:18
  41.1 5.7 %collective-permute-done.6 = f32[128]{0:T(128)S(1)} collective-permute-done((f32[128]{0:T(128)S(1)}, f32[128]{0:T(128)S(1)}, u32[]{:S(2)}, u32[]{:S(2)}) %collective-permute-start.6) | collective-permute-done | bytes 544 | tf_op jit(solution)/shard_map/ppermute | solution.py:18
  46.8 14.3 %all-gather.2.cloned.1.call-done = f32[2048,192]{1,0:T(8,128)} async-done(((f32[128,192]{1,0:T(8,128)}), f32[2048,192]{1,0:T(8,128)}) %all-gather.2.cloned.1.call-update) | async-done | bytes 1572880 | tf_op jit(solution)/shard_map/all_gather | solution.py:9
  61.2 1.7 multiply_reduce_fusion
  62.9 2.2 convolution_multiply_fusion.3
  65.2 1.1 fusion.2
  66.2 1.3 fusion.67
  67.5 2.2 convolution_add_fusion.5
  69.7 2.0 collective-permute-start.13
  71.7 1.0 convolution_multiply_fusion.1
  72.7 1.0 convolution_multiply_fusion.2
  73.7 1.0 convolution_multiply_fusion
  74.7 1.5 convolution_add_fusion.3
  76.2 1.5 convolution_add_fusion.2
  77.7 1.5 convolution_add_fusion.1
  79.2 2.2 fusion.15
  81.4 2.5 collective-permute-start.14
  83.8 1.5 fusion.3
  85.3 0.8 copy.28
  86.2 4.3 %all-to-all-start = ((f32[16,128,64]{1,2,0:T(8,128)}), f32[16,128,64]{1,2,0:T(8,128)}, u32[]{:S(2)}, u32[]{:S(2)}) async-start(f32[16,128,64]{1,2,0:T(8,128)} %bitcast.82), calls=%async_computation | async-start | bytes 1048576 | tf_op jit(solution)/shard_map/all_to_all | solution.py:29
  90.7 2.2 fusion.18
  92.9 2.1 collective-permute-start.15
  95.0 0.8 fusion.68
  96.5 6.6 %all-to-all-done = f32[16,128,64]{1,2,0:T(8,128)} async-done(((f32[16,128,64]{1,2,0:T(8,128)}), f32[16,128,64]{1,2,0:T(8,128)}, u32[]{:S(2)}, u32[]{:S(2)}) %all-to-all-start) | async-done | bytes 524320 | tf_op jit(solution)/shard_map/all_to_all | solution.py:29
  103.1 1.1 reduce_sum.29
  106.7 135.4 %all-reduce.5.cloned.1.call-done = (f32[64,64]{0,1:T(8,128)}, f32[64,64]{1,0:T(8,128)}, f32[64,64]{1,0:T(8,128)}, f32[64,64]{1,0:T(8,128)}) async-done(((f32[64,64]{0,1:T(8,128)}, f32[64,64]{1,0:T(8,128)}, f32[64,64]{1,0:T(8,128)}, f32[64,64]{1,0:T(8,128)}), (f32[64,64]{0,1:T(8,128)}, f32[64,64]{1,0:T(8,128)}, f32[64,64]{1,0:T(8,128)}, f32[64,64]{1,0:T(8,128)})) %all-reduce.5.cloned.1.call-update) | async-done | bytes 65552 | tf_op jit(solution)/shard_map/psum | solution.py:91
  242.2 77.6 %all-reduce.7.cloned.1.call-done = (f32[64,64]{0,1:T(8,128)}, f32[64,64]{1,0:T(8,128)}, f32[64,64]{1,0:T(8,128)}, f32[64,64]{1,0:T(8,128)}) async-done(((f32[64,64]{0,1:T(8,128)}, f32[64,64]{1,0:T(8,128)}, f32[64,64]{1,0:T(8,128)}, f32[64,64]{1,0:T(8,128)}), (f32[64,64]{0,1:T(8,128)}, f32[64,64]{1,0:T(8,128)}, f32[64,64]{1,0:T(8,128)}, f32[64,64]{1,0:T(8,128)})) %all-reduce.7.cloned.1.call-update) | async-done | bytes 65552 | tf_op jit(solution)/shard_map/psum | solution.py:92
  319.8 0.8 copy.19
  321.5 5.8 %cholesky.44 = f32[64,64]{1,0:T(8,128)S(1)} custom-call(f32[64,64]{1,0:T(8,128)S(1)} %fusion.58), custom_call_target="Cholesky" | custom-call | tf_op jit(solution)/shard_map/jit(cholesky)/cholesky | solution.py:59
  328.7 4.9 %custom-call.8 = f32[1,64,64]{1,2,0:T(8,128)S(1)} custom-call(f32[1,64,64]{2,1,0:T(8,128)S(1)} %fusion.47), custom_call_target="InvertDiagBlocksLowerTriangular" | custom-call | tf_op jit(solution)/shard_map/jit(_cho_solve)/triangular_solve | solution.py:60
  333.6 0.8 copy.22
  334.4 1.0 fusion.56
  335.8 1.0 fusion.70
  336.8 0.9 fusion.72
  337.9 0.9 fusion.5
  339.5 5.8 %cholesky.55 = f32[64,64]{1,0:T(8,128)S(1)} custom-call(f32[64,64]{1,0:T(8,128)S(1)} %fusion.53), custom_call_target="Cholesky" | custom-call | tf_op jit(solution)/shard_map/jit(cholesky)/cholesky | solution.py:59
  346.7 4.9 %custom-call.9 = f32[1,64,64]{1,2,0:T(8,128)S(1)} custom-call(f32[1,64,64]{2,1,0:T(8,128)S(1)} %fusion.48), custom_call_target="InvertDiagBlocksLowerTriangular" | custom-call | tf_op jit(solution)/shard_map/jit(_cho_solve)/triangular_solve | solution.py:60
  351.6 1.0 convolution_add_fusion.4
  353.0 0.9 fusion.4
  (57 shorter events, 8.8 us)
Async XLA Ops:
  7.2 54.0 %all-gather.2.cloned.1.call-start = ((), (), s32[]{:S(2)}) async-start(), calls=%async_computation.1 | async-start | bytes 2228224 | tf_op jit(solution)/shard_map/all_gather | solution.py:9
  9.7 6.4 %collective-permute-start.1 = (f32[128,128]{1,0:T(8,128)S(1)}, f32[128,128]{1,0:T(8,128)S(1)}, u32[]{:S(2)}, u32[]{:S(2)}) collective-permute-start(f32[128,128]{1,0:T(8,128)S(1)} %get-tuple-element.14), channel_id=1, source_target_pairs={{0,16},{16,32},{32,48},{48,64},{64,80},{80,96},{96,112},{112,0},{1... | collective-permute-start | bytes 196616 | tf_op jit(solution)/shard_map/ppermute | solution.py:18
  16.2 6.7 %collective-permute-start.4 = (f32[128,128]{1,0:T(8,128)S(1)}, f32[128,128]{1,0:T(8,128)S(1)}, u32[]{:S(2)}, u32[]{:S(2)}) collective-permute-start(f32[128,128]{1,0:T(8,128)S(1)} %collective-permute-done.1), channel_id=1, source_target_pairs={{0,16},{16,32},{32,48},{48,64},{64,80},{80,96},{96,112},{112,0},{1... | collective-permute-start | bytes 196616 | tf_op jit(solution)/shard_map/ppermute | solution.py:18
  16.2 6.7 %collective-permute-start.2 = (f32[128,64]{0,1:T(8,128)}, f32[128,64]{0,1:T(8,128)S(1)}, u32[]{:S(2)}, u32[]{:S(2)}) collective-permute-start(f32[128,64]{0,1:T(8,128)} %param.14), channel_id=1, source_target_pairs={{0,16},{16,32},{32,48},{48,64},{64,80},{80,96},{96,112},{112,0},{1... | collective-permute-start | bytes 98312 | tf_op jit(solution)/shard_map/ppermute | solution.py:18
  22.9 6.4 %collective-permute-start.5 = (f32[128,64]{0,1:T(8,128)S(1)}, f32[128,64]{0,1:T(8,128)S(1)}, u32[]{:S(2)}, u32[]{:S(2)}) collective-permute-start(f32[128,64]{0,1:T(8,128)S(1)} %collective-permute-done.2), channel_id=1, source_target_pairs={{0,16},{16,32},{32,48},{48,64},{64,80},{80,96},{96,112},{112,0},{1... | collective-permute-start | bytes 98312 | tf_op jit(solution)/shard_map/ppermute | solution.py:18
  22.9 23.9 %collective-permute-start.7 = (f32[128,128]{1,0:T(8,128)S(1)}, f32[128,128]{1,0:T(8,128)S(1)}, u32[]{:S(2)}, u32[]{:S(2)}) collective-permute-start(f32[128,128]{1,0:T(8,128)S(1)} %collective-permute-done.4), channel_id=1, source_target_pairs={{0,16},{16,32},{32,48},{48,64},{64,80},{80,96},{96,112},{112,0},{1... | collective-permute-start | bytes 196616 | tf_op jit(solution)/shard_map/ppermute | solution.py:18
  29.3 17.5 %collective-permute-start.8 = (f32[128,64]{0,1:T(8,128)S(1)}, f32[128,64]{0,1:T(8,128)S(1)}, u32[]{:S(2)}, u32[]{:S(2)}) collective-permute-start(f32[128,64]{0,1:T(8,128)S(1)} %collective-permute-done.5), channel_id=1, source_target_pairs={{0,16},{16,32},{32,48},{48,64},{64,80},{80,96},{96,112},{112,0},{1... | collective-permute-start | bytes 98312 | tf_op jit(solution)/shard_map/ppermute | solution.py:18
  29.3 6.1 %collective-permute-start = (f32[128]{0:T(128)S(1)}, f32[128]{0:T(128)S(1)}, u32[]{:S(2)}, u32[]{:S(2)}) collective-permute-start(f32[128]{0:T(128)S(1)} %get-tuple-element.13), channel_id=1, source_target_pairs={{0,16},{16,32},{32,48},{48,64},{64,80},{80,96},{96,112},{112,0},{1... | collective-permute-start | bytes 1544 | tf_op jit(solution)/shard_map/ppermute | solution.py:18
  35.4 5.7 %collective-permute-start.3 = (f32[128]{0:T(128)S(1)}, f32[128]{0:T(128)S(1)}, u32[]{:S(2)}, u32[]{:S(2)}) collective-permute-start(f32[128]{0:T(128)S(1)} %collective-permute-done), channel_id=1, source_target_pairs={{0,16},{16,32},{32,48},{48,64},{64,80},{80,96},{96,112},{112,0},{1... | collective-permute-start | bytes 1544 | tf_op jit(solution)/shard_map/ppermute | solution.py:18
  41.1 5.7 %collective-permute-start.6 = (f32[128]{0:T(128)S(1)}, f32[128]{0:T(128)S(1)}, u32[]{:S(2)}, u32[]{:S(2)}) collective-permute-start(f32[128]{0:T(128)S(1)} %collective-permute-done.3), channel_id=1, source_target_pairs={{0,16},{16,32},{32,48},{48,64},{64,80},{80,96},{96,112},{112,0},{1... | collective-permute-start | bytes 1544 | tf_op jit(solution)/shard_map/ppermute | solution.py:18
  41.1 26.4 %collective-permute-start.12 = (f32[128,64]{0,1:T(8,128)S(1)}, f32[128,64]{0,1:T(8,128)S(1)}, u32[]{:S(2)}, u32[]{:S(2)}) collective-permute-start(f32[128,64]{0,1:T(8,128)S(1)} %broadcast_in_dim.2), channel_id=1, source_target_pairs={{0,16},{16,32},{32,48},{48,64},{64,80},{80,96},{96,112},{112,0},{1... | collective-permute-start | bytes 98312 | tf_op jit(solution)/shard_map/ppermute | solution.py:18
  46.7 37.1 %collective-permute-start.9 = (f32[128]{0:T(128)S(1)}, f32[128]{0:T(128)S(1)}, u32[]{:S(2)}, u32[]{:S(2)}) collective-permute-start(f32[128]{0:T(128)S(1)} %collective-permute-done.6), channel_id=1, source_target_pairs={{0,16},{16,32},{32,48},{48,64},{64,80},{80,96},{96,112},{112,0},{1... | collective-permute-start | bytes 1544 | tf_op jit(solution)/shard_map/ppermute | solution.py:18
  46.7 37.1 %collective-permute-start.11 = (f32[128,64]{0,1:T(8,128)S(1)}, f32[128,64]{0,1:T(8,128)S(1)}, u32[]{:S(2)}, u32[]{:S(2)}) collective-permute-start(f32[128,64]{0,1:T(8,128)S(1)} %collective-permute-done.8), channel_id=1, source_target_pairs={{0,16},{16,32},{32,48},{48,64},{64,80},{80,96},{96,112},{112,0},{1... | collective-permute-start | bytes 98312 | tf_op jit(solution)/shard_map/ppermute | solution.py:18
  46.8 26.9 %collective-permute-start.10 = (f32[128,128]{1,0:T(8,128)S(1)}, f32[128,128]{1,0:T(8,128)S(1)}, u32[]{:S(2)}, u32[]{:S(2)}) collective-permute-start(f32[128,128]{1,0:T(8,128)S(1)} %collective-permute-done.7), channel_id=1, source_target_pairs={{0,16},{16,32},{32,48},{48,64},{64,80},{80,96},{96,112},{112,0},{1... | collective-permute-start | bytes 196616 | tf_op jit(solution)/shard_map/ppermute | solution.py:18
  61.2 4.0 %copy-start = (f32[2048,192]{1,0:T(8,128)S(1)}, f32[2048,192]{1,0:T(8,128)}, u32[]{:S(2)}) copy-start(f32[2048,192]{1,0:T(8,128)} %all-gather.2.cloned.1.call-done) | copy-start | bytes 4718596
  62.9 3.3 copy-start.1
  69.7 9.5 %collective-permute-start.13 = (f32[128,64]{0,1:T(8,128)S(1)}, f32[128,64]{0,1:T(8,128)S(1)}, u32[]{:S(2)}, u32[]{:S(2)}) collective-permute-start(f32[128,64]{0,1:T(8,128)S(1)} %convolution_add_fusion.5), channel_id=1, source_target_pairs={{0,16},{16,32},{32,48},{48,64},{64,80},{80,96},{96,112},{112,0},{1... | collective-permute-start | bytes 98312 | tf_op jit(solution)/shard_map/ppermute | solution.py:18
  81.4 9.4 %collective-permute-start.14 = (f32[128,64]{0,1:T(8,128)S(1)}, f32[128,64]{0,1:T(8,128)S(1)}, u32[]{:S(2)}, u32[]{:S(2)}) collective-permute-start(f32[128,64]{0,1:T(8,128)S(1)} %fusion.15), channel_id=1, source_target_pairs={{0,16},{16,32},{32,48},{48,64},{64,80},{80,96},{96,112},{112,0},{1... | collective-permute-start | bytes 98312 | tf_op jit(solution)/shard_map/ppermute | solution.py:18
  85.3 9.7 %copy-start.2 = (f32[128,64]{0,1:T(8,128)S(1)}, f32[128,64]{0,1:T(8,128)}, u32[]{:S(2)}) copy-start(f32[128,64]{0,1:T(8,128)} %param.13) | copy-start | bytes 98308
  86.2 17.0 %all-to-all-start = ((f32[16,128,64]{1,2,0:T(8,128)}), f32[16,128,64]{1,2,0:T(8,128)}, u32[]{:S(2)}, u32[]{:S(2)}) async-start(f32[16,128,64]{1,2,0:T(8,128)} %bitcast.82), calls=%async_computation | async-start | bytes 1048576 | tf_op jit(solution)/shard_map/all_to_all | solution.py:29
  90.4 247.4 %copy-start.4 = (f32[128,64]{0,1:T(8,128)S(1)}, f32[128,64]{0,1:T(8,128)}, u32[]{:S(2)}) copy-start(f32[128,64]{0,1:T(8,128)} %param.12) | copy-start | bytes 98308
  90.5 151.7 %all-reduce.5.cloned.1.call-start = ((), (), s32[]{:S(2)}) async-start(), calls=%async_computation.2 | async-start | bytes 262144 | tf_op jit(solution)/shard_map/psum | solution.py:91
  92.9 11.3 %collective-permute-start.15 = (f32[128,64]{0,1:T(8,128)S(1)}, f32[128,64]{0,1:T(8,128)S(1)}, u32[]{:S(2)}, u32[]{:S(2)}) collective-permute-start(f32[128,64]{0,1:T(8,128)S(1)} %fusion.18), channel_id=1, source_target_pairs={{0,80},{16,96},{32,112},{48,0},{64,16},{80,32},{96,48},{112,64},{1... | collective-permute-start | bytes 98312 | tf_op jit(solution)/shard_map/ppermute | solution.py:18
  106.7 213.1 %all-reduce.7.cloned.1.call-start = ((), (), s32[]{:S(2)}) async-start(), calls=%async_computation.3 | async-start | bytes 262144 | tf_op jit(solution)/shard_map/psum | solution.py:92
  335.8 18.0 %copy-start.3 = (f32[128,64]{0,1:T(8,128)}, f32[128,64]{0,1:T(8,128)S(1)}, u32[]{:S(2)}) copy-start(f32[128,64]{0,1:T(8,128)S(1)} %convolution_subtract_fusion) | copy-start | bytes 98308
Sparse Core Ops, SparseCore 0:
  10.4 50.6 all-gather.1
  106.8 135.3 all-reduce.4
  244.9 74.8 all-reduce.6
